TPU v7x, 32 devices: a whole 2x2x4 slice. The times are simulated.
32 devices in a mesh: tp: 4 (over z), cp: 2 (over y), dp: 4 (over x, core).
Axes of the slice: x: 2, y: 2, z: 4, core: 2. Of those that a mesh axis runs over, the one named last changes fastest.
Arguments:
- hidden: bfloat16 [128, 64, 2048], P('dp', 'cp')
- tokens: int32 [128, 64], P('dp', 'cp')
- seq_lens: int32 [128], P('dp')
- norm_gain: float32 [2048], replicated
- w_head: bfloat16 [2048, 49152], P(None, 'tp')
Outputs:
- output 1: float32 [128, 64], P('dp', 'cp')
- output 2: float32 [], replicated
- output 3: bfloat16 [128, 64, 2048], P('dp', 'cp')
- output 4: float32 [2048], replicated
- output 5: float32 [2048, 49152], P(None, 'tp')
All inputs are finite; a program needn't handle non-finite values.
Results may differ from a plain program's by a relative error of at most 0.001.
Values sent between devices are 32-bit elements.
A program may use at most 1 GiB of HBM per device.

v0:
```python
import jax
import jax.numpy as jnp
from jax import lax
from jax.sharding import PartitionSpec as P

NORM_EPS = 1e-5


def solution(mesh):
    cp_size = mesh.shape['cp']
    from_next_pairs = [(cp_idx + 1, cp_idx) for cp_idx in range(cp_size - 1)]
    from_prev_pairs = [(cp_idx - 1, cp_idx) for cp_idx in range(1, cp_size)]

    def local_fn(hidden, tokens, seq_lens, norm_gain, w_head):
        local_len = tokens.shape[1]
        seg_len = local_len // 2
        vocab_local = w_head.shape[1]
        cp_rank = lax.axis_index('cp')
        tp_rank = lax.axis_index('tp')

        next_first = lax.ppermute(tokens[:, 0], 'cp', from_next_pairs)
        prev_second = lax.ppermute(tokens[:, seg_len], 'cp', from_prev_pairs)
        first_end = jnp.where(cp_rank == cp_size - 1, tokens[:, seg_len], next_first)
        labels = jnp.concatenate([tokens[:, 1:seg_len], first_end[:, None], tokens[:, seg_len + 1:], prev_second[:, None]], axis=1)

        seg_pos = jnp.arange(seg_len)
        positions = jnp.concatenate([cp_rank * seg_len + seg_pos, (2 * cp_size - 1 - cp_rank) * seg_len + seg_pos])
        valid_mask = (positions[None, :] + 1 < seq_lens[:, None]).astype(jnp.float32)
        valid_count = lax.psum(jnp.sum(seq_lens - 1).astype(jnp.float32), 'dp')

        h_f32 = hidden.astype(jnp.float32)
        inv_rms = lax.rsqrt(jnp.mean(h_f32 * h_f32, axis=-1, keepdims=True) + NORM_EPS)
        x_hat = h_f32 * inv_rms
        x_norm = (x_hat * norm_gain).astype(jnp.bfloat16)
        logits = jnp.einsum('bsd,dv->bsv', x_norm, w_head, preferred_element_type=jnp.float32)

        glob_max = lax.pmax(jnp.max(logits, axis=-1), 'tp')
        sum_exp = lax.psum(jnp.sum(jnp.exp(logits - glob_max[..., None]), axis=-1), 'tp')
        log_norm = glob_max + jnp.log(sum_exp)
        local_lab = labels - tp_rank * vocab_local
        label_hit = jnp.arange(vocab_local)[None, None, :] == local_lab[..., None]
        target_logit = lax.psum(jnp.sum(jnp.where(label_hit, logits, 0.0), axis=-1), 'tp')
        tok_loss = (log_norm - target_logit) * valid_mask
        loss_mean = lax.psum(jnp.sum(tok_loss), ('cp', 'dp')) / valid_count

        tok_scale = valid_mask / valid_count
        soft_prob = jnp.exp(logits - log_norm[..., None])
        d_logits = ((soft_prob - label_hit.astype(jnp.float32)) * tok_scale[..., None]).astype(jnp.bfloat16)
        dx_norm = lax.psum(jnp.einsum('bsv,dv->bsd', d_logits, w_head, preferred_element_type=jnp.float32), 'tp')
        d_head = lax.psum(jnp.einsum('bsd,bsv->dv', x_norm, d_logits, preferred_element_type=jnp.float32), ('cp', 'dp'))
        d_gain = lax.psum(jnp.sum(dx_norm * x_hat, axis=(0, 1)), ('cp', 'dp'))
        dx_hat = dx_norm * norm_gain
        d_hidden = (inv_rms * (dx_hat - x_hat * jnp.mean(dx_hat * x_hat, axis=-1, keepdims=True))).astype(jnp.bfloat16)
        return tok_loss, loss_mean, d_hidden, d_gain, d_head

    return jax.shard_map(local_fn, mesh=mesh, in_specs=(P('dp', 'cp', None), P('dp', 'cp'), P('dp'), P(None), P(None, 'tp')), out_specs=(P('dp', 'cp'), P(), P('dp', 'cp', None), P(None), P(None, 'tp')), check_vma=False)
```

profile of v0, /device:TPU:1, one launch (start us, length us, event | category | flops | bytes accessed | tf_op | source)
XLA Modules:
  0.0 1704.7 jit_solution(13353831269365297050)
XLA Ops:
  7.2 0.0 all-reduce.5.cloned.1.call-start
  7.2 1.5 slice_reduce_fusion
  8.7 1.3 collective-permute-start
  10.0 5.1 collective-permute-start.1
  15.1 1.5 fusion.19
  16.6 1.3 add_reduce_fusion
  18.5 7.5 psum.52
  26.0 3.1 fusion.14
  29.1 0.0 copy-start
  29.1 0.0 copy-start.1
  29.1 61.0 %fusion.20 = (f32[32,32]{1,0:T(8,128)S(1)}, f32[32,32,12288]{2,1,0:T(8,128)}) fusion(bf16[2048,12288]{1,0:T(8,128)(2,1)} %param.9, bf16[32,32,2048]{2,1,0:T(8,128)(2,1)} %param.5, f32[2048]{0:T(1024)} %param.8, f32[32,32]{1,0:T(8,128)S(1)} %add_rsqrt_fusion), kind=kOutput, calls=%fused_computation.38 | convolution fusion | flops 51560579072 | bytes 104873984 | tf_op jit(solution)/shard_map/bsd,dv->bsv/dot_general | solution.py:35
  90.2 15.4 pmax.7
  105.5 0.1 add_add_fusion
  106.3 0.0 collective-permute-done.1
  106.3 0.7 copy.13
  107.1 0.6 fusion.17
  107.7 0.1 copy.12
  107.8 0.1 add_subtract_fusion
  107.9 23.1 %select_reduce_fusion = (f32[32,32]{1,0:T(8,128)S(1)}, f32[32,32]{1,0:T(8,128)S(1)}) fusion(f32[32,32,12288]{2,1,0:T(8,128)} %get-tuple-element.22, s32[32,32]{1,0:T(8,128)S(1)} %add_subtract_fusion, f32[32,32]{1,0:T(8,128)S(1)} %pmax.7), kind=kLoop, calls=%fused_computation.6 | loop fusion | flops 62912512 | bytes 50348032 | tf_op jit(solution)/shard_map/reduce_sum | solution.py:42
  131.1 12.5 all-reduce.1
  143.6 1.3 fusion.18
  144.8 64.7 %fusion = f32[32,32,2048]{2,1,0:T(8,128)} fusion(bf16[2048,12288]{1,0:T(8,128)(2,1)} %param.9, f32[32,32,12288]{2,1,0:T(8,128)} %get-tuple-element.22, f32[32,32]{1,0:T(8,128)S(1)} %get-tuple-element.20, f32[32,32]{1,0:T(8,128)S(1)} %get-tuple-element.17, s32[32,32]{1,0:T(8,128)S(1)} %add_subtract_fusion), kind=kOutput, calls=%fused_computation.1 | convolution fusion | flops 51615105024 | bytes 109064192 | tf_op jit(solution)/shard_map/bsv,dv->bsd/dot_general | solution.py:49
  209.5 0.0 all-reduce.5.cloned.1.call-update
  209.6 0.3 all-reduce.7.cloned.1.call-start
  209.8 70.3 %convolution_bitcast_fusion = f32[2048,12288]{1,0:T(8,128)} fusion(bf16[32,32,2048]{2,1,0:T(8,128)(2,1)} %param.5, f32[2048]{0:T(1024)S(1)} %copy-done.2, f32[32,32]{1,0:T(8,128)S(1)} %add_rsqrt_fusion, f32[32,32,12288]{2,1,0:T(8,128)} %get-tuple-element.22, f32[32,32]{1,0:T(8,128)S(1)} %get-tuple-element.20, f32[32,32]{1,0:T(8,128)S(1)} %get-tuple-element.17, ...), kind=kOutput, calls=%fused_computation | convolution fusion | flops 51623493632 | bytes 155213824 | tf_op jit(solution)/shard_map/bsd,bsv->dv/dot_general | solution.py:50
  280.1 0.0 all-reduce.7.cloned.1.call-update
  280.1 223.8 %all-reduce.5.cloned.1.call-done = f32[32,32,2048]{2,1,0:T(8,128)} async-done(((f32[32,32,2048]{2,1,0:T(8,128)}), f32[32,32,2048]{2,1,0:T(8,128)}) %all-reduce.5.cloned.1.call-update) | async-done | bytes 8388624 | tf_op jit(solution)/shard_map/psum | solution.py:49
  503.9 5.9 fusion.13
  509.8 13.9 all-reduce
  525.0 7.0 fusion.12
  532.0 1099.1 %all-reduce.7.cloned.1.call-done = f32[2048,12288]{1,0:T(8,128)} async-done(((f32[2048,12288]{1,0:T(8,128)}), f32[2048,12288]{1,0:T(8,128)}) %all-reduce.7.cloned.1.call-update) | async-done | bytes 100663312 | tf_op jit(solution)/shard_map/psum | solution.py:50
  1631.1 65.7 %copy.16 = f32[2048,12288]{1,0:T(8,128)} copy(f32[2048,12288]{1,0:T(8,128)} %all-reduce.7.cloned.1.call-done) | data formatting | bytes 201326592
  (10 shorter events, 0.0 us)
Async XLA Ops:
  7.2 496.7 %all-reduce.5.cloned.1.call-start = ((), (), s32[]{:S(2)}) async-start(), calls=%async_computation | async-start | bytes 16777216 | tf_op jit(solution)/shard_map/psum | solution.py:49
  8.7 98.4 %collective-permute-start = (s32[32]{0:T(128)}, s32[32]{0:T(128)}, u32[]{:S(2)}, u32[]{:S(2)}) collective-permute-start(s32[32]{0:T(128)} %get-tuple-element.9), channel_id=1, source_target_pairs={{4,0},{5,1},{6,2},{7,3},{12,8},{13,9},{14,10},{15,11},{20,16},{21,... | collective-permute-start | bytes 392 | tf_op jit(solution)/shard_map/ppermute | solution.py:21
  10.0 96.3 %collective-permute-start.1 = (s32[32]{0:T(128)}, s32[32]{0:T(128)}, u32[]{:S(2)}, u32[]{:S(2)}) collective-permute-start(s32[32]{0:T(128)} %get-tuple-element.10), channel_id=1, source_target_pairs={{0,4},{1,5},{2,6},{3,7},{8,12},{9,13},{10,14},{11,15},{16,20},{17,... | collective-permute-start | bytes 392 | tf_op jit(solution)/shard_map/ppermute | solution.py:22
  29.1 78.7 %copy-start = (s32[32,15]{1,0:T(8,128)S(1)}, s32[32,15]{1,0:T(8,128)}, u32[]{:S(2)}) copy-start(s32[32,15]{1,0:T(8,128)} %get-tuple-element.18) | copy-start | bytes 5764
  29.1 78.7 %copy-start.1 = (s32[32,15]{1,0:T(8,128)S(1)}, s32[32,15]{1,0:T(8,128)}, u32[]{:S(2)}) copy-start(s32[32,15]{1,0:T(8,128)} %get-tuple-element.19) | copy-start | bytes 5764
  107.9 35.6 %copy-start.3 = (s32[32]{0:T(128)S(1)}, s32[32]{0:T(128)}, u32[]{:S(2)}) copy-start(s32[32]{0:T(128)} %param.7) | copy-start | bytes 388
  144.8 65.0 %copy-start.2 = (f32[2048]{0:T(1024)S(1)}, f32[2048]{0:T(1024)}, u32[]{:S(2)}) copy-start(f32[2048]{0:T(1024)} %param.8) | copy-start | bytes 24580
  209.6 1421.6 %all-reduce.7.cloned.1.call-start = ((), (), s32[]{:S(2)}) async-start(), calls=%async_computation.1 | async-start | bytes 201326592 | tf_op jit(solution)/shard_map/psum | solution.py:50
Sparse Core Ops, SparseCore 0:
  209.7 294.1 all-reduce.4
  508.3 1122.7 all-reduce.6
where the time goes:
time: 1710 us; the launch traced here: 1700 us
  waiting for transfers between devices  1320 us (77%)
  matrix products  196 us (11%)
  local copies, waits for them, and re-layouts  69.5 us (4%)
  blocking collectives  49.3 us (3%)
  other arithmetic  42.4 us (2%)
  between operations  18 us (1%)
    psum x1, waiting for transfers between devices, local_fn(): lax.psum(jnp.einsum('bsd,bsv->dv', x_norm, d_logits, preferred_element_ty...  1100 us
    psum x1, waiting for transfers between devices, local_fn(): lax.psum(jnp.einsum('bsv,dv->bsd', d_logits, w_head, preferred_element_ty...  224 us
    dot_general x1, matrix products, local_fn(): jnp.einsum('bsd,bsv->dv', x_norm, d_logits, preferred_element_type=jnp.fl...  70.3 us
    unnamed x9, local copies, waits for them, and re-layouts  65.7 us
    dot_general x1, matrix products, local_fn(): jnp.einsum('bsv,dv->bsd', d_logits, w_head, preferred_element_type=jnp.fl...  64.7 us
    dot_general x1, matrix products, local_fn(): jnp.einsum('bsd,dv->bsv', x_norm, w_head, preferred_element_type=jnp.floa...  61 us
  transfers between devices with their start and end apart: 4, of which 2 were waited for; matrix products, arithmetic and copies ran while one was open for 9% of the time, Pallas kernels for 0%

commit v1 on v0

v1 whole, which is shorter than its diff:
```python
import jax
import jax.numpy as jnp
from jax import lax
from jax.sharding import PartitionSpec as P
from jax.experimental import pallas as pl
from jax.experimental.pallas import tpu as pltpu

NORM_EPS = 1e-5
F32, BF16 = jnp.float32, jnp.bfloat16
N_COL = 8
TOK = 1024
VMEM = 64_000_000


def _params(**kw):
    return pltpu.CompilerParams(vmem_limit_bytes=VMEM, **kw)


def _cost(flops, bytes_accessed):
    return pl.CostEstimate(flops=int(flops), bytes_accessed=int(bytes_accessed), transcendentals=0)


def _norm(hidden, gain):
    rows, width = hidden.shape
    step = 256

    def kernel(h_ref, g_ref, x_ref, xs_ref):
        h = h_ref[...].astype(F32)
        inv_rms = lax.rsqrt(jnp.mean(h * h, axis=-1, keepdims=True) + NORM_EPS)
        x = (h * inv_rms * g_ref[...]).astype(BF16)
        x_ref[...] = x
        xs_ref[...] = x.astype(F32)

    return pl.pallas_call(
        kernel,
        grid=(rows // step,),
        out_shape=[jax.ShapeDtypeStruct((rows, width), BF16), jax.ShapeDtypeStruct((rows, width), F32)],
        in_specs=[pl.BlockSpec((step, width), lambda i: (i, 0)), pl.BlockSpec((1, width), lambda i: (0, 0))],
        out_specs=[pl.BlockSpec((step, width), lambda i: (i, 0)), pl.BlockSpec((step, width), lambda i: (i, 0))],
        compiler_params=_params(),
        cost_estimate=_cost(rows * width * 256, rows * width * 8),
    )(hidden, gain)


def _logits(x, labels, w):
    rows, width = x.shape
    vocab = w.shape[1]
    cols = 1024
    steps = vocab // cols

    def kernel(x_ref, lab_ref, w_ref, z_ref, st_ref, m_ref, s_ref, t_ref):
        i = pl.program_id(0)

        @pl.when(i == 0)
        def _():
            m_ref[...] = jnp.full_like(m_ref, -jnp.inf)
            s_ref[...] = jnp.zeros_like(s_ref)
            t_ref[...] = jnp.zeros_like(t_ref)

        z = jnp.dot(x_ref[...], w_ref[...], preferred_element_type=F32)
        z_ref[...] = z
        rel = lab_ref[...] - cols * i
        lane = lax.broadcasted_iota(jnp.int32, (rows, 128), 1)
        old = m_ref[...]
        top = old
        for g in range(cols // 128):
            top = jnp.maximum(top, z[:, g * 128:(g + 1) * 128])
        total = s_ref[...] * jnp.exp(old - top)
        target = t_ref[...]
        for g in range(cols // 128):
            z_g = z[:, g * 128:(g + 1) * 128]
            total = total + jnp.exp(z_g - top)
            target = target + jnp.where(lane == rel - g * 128, z_g, 0.0)
        m_ref[...] = top
        s_ref[...] = total
        t_ref[...] = target

        @pl.when(i == steps - 1)
        def _():
            row_max = jnp.max(top, axis=1, keepdims=True)
            row_sum = jnp.sum(total * jnp.exp(top - row_max), axis=1, keepdims=True)
            row_target = jnp.sum(target, axis=1, keepdims=True)
            st_ref[...] = jnp.where(lane == 0, row_max, jnp.where(lane == 1, row_sum, row_target))

    return pl.pallas_call(
        kernel,
        grid=(steps,),
        out_shape=[jax.ShapeDtypeStruct((rows, vocab), F32), jax.ShapeDtypeStruct((rows, 128), F32)],
        in_specs=[pl.BlockSpec((rows, width), lambda i: (0, 0)), pl.BlockSpec((rows, 1), lambda i: (0, 0)), pl.BlockSpec((width, cols), lambda i: (0, i))],
        out_specs=[pl.BlockSpec((rows, cols), lambda i: (0, i)), pl.BlockSpec((rows, 128), lambda i: (0, 0))],
        scratch_shapes=[pltpu.VMEM((rows, 128), F32)] * 3,
        compiler_params=_params(),
        cost_estimate=_cost(2 * rows * width * vocab, vocab * (2 * width + 4 * rows)),
    )(x, labels, w)


def _d_logits(z, meta, first):
    rel = meta[:, 1:2].astype(jnp.int32) - first
    hit = lax.broadcasted_iota(jnp.int32, z.shape, 1) == rel
    return ((jnp.exp(z - meta[:, 0:1]) - jnp.where(hit, 1.0, 0.0)) * meta[:, 2:3]).astype(BF16)


def _d_norm(z, meta, w):
    rows, vocab = z.shape
    width = w.shape[0]
    cols = 1024

    def kernel(z_ref, meta_ref, w_ref, acc_ref):
        i = pl.program_id(0)

        @pl.when(i == 0)
        def _():
            acc_ref[...] = jnp.zeros_like(acc_ref)

        d = _d_logits(z_ref[...], meta_ref[...], lax.axis_index('tp') * vocab + i * cols)
        acc_ref[...] += lax.dot_general(d, w_ref[...], (((1,), (1,)), ((), ())), preferred_element_type=F32)

    return pl.pallas_call(
        kernel,
        grid=(vocab // cols,),
        out_shape=jax.ShapeDtypeStruct((rows, width), F32),
        in_specs=[pl.BlockSpec((rows, cols), lambda i: (0, i)), pl.BlockSpec((rows, 4), lambda i: (0, 0)), pl.BlockSpec((width, cols), lambda i: (0, i))],
        out_specs=pl.BlockSpec((rows, width), lambda i: (0, 0)),
        compiler_params=_params(),
        cost_estimate=_cost(2 * rows * width * vocab, vocab * (2 * width + 4 * rows)),
    )(z, meta, w)


def _d_head_first(x, meta, w, cols):
    rows, width = x.shape
    vocab = w.shape[1]
    half = vocab // 2

    def kernel(x_ref, meta_ref, w_ref, acc_ref):
        first = lax.axis_index('tp') * vocab + lax.axis_index('dp') % 2 * half + pl.program_id(0) * cols

        @pl.when(pl.program_id(1) == 0)
        def _():
            acc_ref[...] = jnp.zeros_like(acc_ref)

        x_b = x_ref[...].astype(BF16)
        d = _d_logits(jnp.dot(x_b, w_ref[...], preferred_element_type=F32), meta_ref[...], first)
        acc_ref[...] += lax.dot_general(x_b, d, (((0,), (0,)), ((), ())), preferred_element_type=F32)

    return pl.pallas_call(
        kernel,
        grid=(half // cols, rows // TOK),
        out_shape=jax.ShapeDtypeStruct((width, half), F32),
        in_specs=[
            pl.BlockSpec((TOK, width), lambda j, i: (i, 0)),
            pl.BlockSpec((TOK, 4), lambda j, i: (i, 0)),
            pl.BlockSpec((width, cols), lambda j, i: (0, lax.axis_index('dp') % 2 * (half // cols) + j)),
        ],
        out_specs=pl.BlockSpec((width, cols), lambda j, i: (0, j)),
        compiler_params=_params(),
        cost_estimate=_cost(4 * rows * width * half, half // cols * rows * width * 4),
    )(x, meta, w)


def _d_head_last(x, meta, w, first_part, cols):
    rows, width = x.shape
    vocab = w.shape[1]
    half = vocab // 2
    n_col = half // cols
    n_tok = rows // TOK

    def kernel(x_ref, meta_ref, w_ref, init_ref, out_ref, acc_ref, init_sem, own_sem, send_sem, recv_sem):
        j, i = pl.program_id(0), pl.program_id(1)
        me = lax.axis_index('dp')
        core = me % 2
        peer = me + 1 - 2 * core
        slot = j % 2

        def own(jj):
            at = pl.ds(pl.multiple_of(core * half + jj * cols, 128), cols)
            return pltpu.make_async_copy(acc_ref.at[jj % 2], out_ref.at[:, at], own_sem.at[jj % 2])

        def send(jj):
            at = pl.ds(pl.multiple_of(core * half + jj * cols, 128), cols)
            return pltpu.make_async_remote_copy(acc_ref.at[jj % 2], out_ref.at[:, at], send_sem.at[jj % 2], recv_sem.at[jj], device_id={'dp': peer}, device_id_type=pl.DeviceIdType.MESH)

        def arrival(jj):
            at = pl.ds(pl.multiple_of((1 - core) * half + jj * cols, 128), cols)
            return pltpu.make_async_remote_copy(acc_ref.at[jj % 2], out_ref.at[:, at], send_sem.at[jj % 2], recv_sem.at[jj], device_id={'dp': peer}, device_id_type=pl.DeviceIdType.MESH)

        def init(jj):
            return pltpu.make_async_copy(init_ref.at[:, pl.ds(pl.multiple_of(jj * cols, 128), cols)], acc_ref.at[jj % 2], init_sem.at[jj % 2])

        @pl.when((j == 0) & (i == 0))
        def _():
            init(0).start()
            barrier = pltpu.get_barrier_semaphore()
            pl.semaphore_signal(barrier, inc=1, device_id={'dp': peer}, device_id_type=pl.DeviceIdType.MESH)
            pl.semaphore_wait(barrier, 1)

        @pl.when(i == 0)
        def _():
            init(j).wait()

        @pl.when(i == n_tok // 2)
        def _():
            @pl.when(j >= 1)
            def _():
                own(j - 1).wait()
                send(j - 1).wait_send()

            @pl.when(j < n_col - 1)
            def _():
                init(j + 1).start()

        first = lax.axis_index('tp') * vocab + core * half + j * cols
        x_b = x_ref[...].astype(BF16)
        d = _d_logits(jnp.dot(x_b, w_ref[...], preferred_element_type=F32), meta_ref[...], first)
        acc_ref[slot] += lax.dot_general(x_b, d, (((0,), (0,)), ((), ())), preferred_element_type=F32)

        @pl.when(i == n_tok - 1)
        def _():
            own(j).start()
            send(j).start()

        @pl.when((j == n_col - 1) & (i == n_tok - 1))
        def _():
            own(j).wait()
            send(j).wait_send()
            for jj in range(n_col):
                arrival(jj).wait_recv()

    return pl.pallas_call(
        kernel,
        grid=(n_col, n_tok),
        out_shape=jax.ShapeDtypeStruct((width, vocab), F32),
        in_specs=[
            pl.BlockSpec((TOK, width), lambda j, i: (i, 0)),
            pl.BlockSpec((TOK, 4), lambda j, i: (i, 0)),
            pl.BlockSpec((width, cols), lambda j, i: (0, lax.axis_index('dp') % 2 * n_col + j)),
            pl.BlockSpec(memory_space=pl.ANY),
        ],
        out_specs=pl.BlockSpec(memory_space=pl.ANY),
        scratch_shapes=[pltpu.VMEM((2, width, cols), F32)] + [pltpu.SemaphoreType.DMA((2,))] * 3 + [pltpu.SemaphoreType.DMA((n_col,))],
        compiler_params=_params(collective_id=0, has_side_effects=True),
        cost_estimate=_cost(4 * rows * width * half, half // cols * rows * width * 4),
    )(x, meta, w, first_part)


def _finish(hidden, d_x_norm, gain):
    rows, width = hidden.shape
    step = 256

    def kernel(h_ref, d_ref, g_ref, dh_ref, dg_ref):
        @pl.when(pl.program_id(0) == 0)
        def _():
            dg_ref[...] = jnp.zeros_like(dg_ref)

        h = h_ref[...].astype(F32)
        inv_rms = lax.rsqrt(jnp.mean(h * h, axis=-1, keepdims=True) + NORM_EPS)
        x = h * inv_rms
        d = d_ref[...]
        dg_ref[...] += jnp.sum(d * x, axis=0, keepdims=True)
        d_x = d * g_ref[...]
        dh_ref[...] = (inv_rms * (d_x - x * jnp.mean(d_x * x, axis=-1, keepdims=True))).astype(BF16)

    return pl.pallas_call(
        kernel,
        grid=(rows // step,),
        out_shape=[jax.ShapeDtypeStruct((rows, width), BF16), jax.ShapeDtypeStruct((1, width), F32)],
        in_specs=[pl.BlockSpec((step, width), lambda i: (i, 0)), pl.BlockSpec((step, width), lambda i: (i, 0)), pl.BlockSpec((1, width), lambda i: (0, 0))],
        out_specs=[pl.BlockSpec((step, width), lambda i: (i, 0)), pl.BlockSpec((1, width), lambda i: (0, 0))],
        compiler_params=_params(),
        cost_estimate=_cost(rows * width * 256, rows * width * 8),
    )(hidden, d_x_norm, gain)


def solution(mesh):
    n_tp, n_cp, n_dp = mesh.shape['tp'], mesh.shape['cp'], mesh.shape['dp']
    groups = n_cp * n_dp

    def part_fn(hidden, tokens, seq_lens, norm_gain, w_head):
        n_seq, local_len, width = hidden.shape
        n_tok = n_seq * local_len
        half_tok = n_tok // 2
        sub = half_tok // n_tp
        seg_len = local_len // 2
        vocab_local = w_head.shape[1]
        cp_rank = lax.axis_index('cp')
        tp_rank = lax.axis_index('tp')
        me = cp_rank * n_dp + lax.axis_index('dp')
        gain = norm_gain.reshape(1, width)
        hidden_rows = hidden.reshape(n_tok, width)

        x_norm, x_send = _norm(hidden_rows, gain)
        x_a = lax.all_gather(x_send[:half_tok], ('cp', 'dp'), axis=0, tiled=True)
        x_b = lax.all_gather(lax.dynamic_slice_in_dim(x_send, half_tok + tp_rank * sub, sub), ('tp', 'cp', 'dp'), axis=0, tiled=True)

        edge = lax.ppermute(jnp.where(cp_rank == 0, tokens[:, seg_len], tokens[:, 0]), 'cp', [(0, 1), (1, 0)])
        first_end = jnp.where(cp_rank == 0, edge, tokens[:, seg_len])
        second_end = jnp.where(cp_rank == 0, 0, edge)
        labels = jnp.concatenate([tokens[:, 1:seg_len], first_end[:, None], tokens[:, seg_len + 1:], second_end[:, None]], axis=1)
        seg_pos = jnp.arange(seg_len)
        positions = jnp.concatenate([cp_rank * seg_len + seg_pos, (2 * n_cp - 1 - cp_rank) * seg_len + seg_pos])
        valid = (positions[None, :] + 1 < seq_lens[:, None]).astype(F32).reshape(n_tok)
        labels = labels.reshape(n_tok)

        logits, row_stats = _logits(x_norm, (labels - tp_rank * vocab_local).reshape(n_tok, 1), w_head)

        mine = jnp.concatenate([row_stats[:, :3].T, labels.astype(F32)[None], valid[None]])
        stats = lax.all_gather(mine, ('tp', 'cp', 'dp'), axis=0, tiled=False).reshape(n_tp, groups, 5, n_tok)
        all_max = jnp.max(stats[:, :, 0], axis=0)
        all_sum = jnp.sum(stats[:, :, 1] * jnp.exp(stats[:, :, 0] - all_max[None]), axis=0)
        all_lse = all_max + jnp.log(all_sum)
        all_valid = stats[0, :, 4]
        all_loss = (all_lse - jnp.sum(stats[:, :, 2], axis=0)) * all_valid
        valid_count = jnp.sum(all_valid)
        loss_mean = jnp.sum(all_loss) / valid_count
        tok_loss = lax.dynamic_index_in_dim(all_loss, me, 0, keepdims=False).reshape(n_seq, local_len)
        meta = jnp.stack([all_lse, stats[0, :, 3], all_valid / valid_count, all_valid], axis=-1)
        meta_own = lax.dynamic_index_in_dim(meta, me, 0, keepdims=False)
        meta_a = meta[:, :half_tok].reshape(groups * half_tok, 4)
        meta_b = meta[:, half_tok:].reshape(groups, n_tp, sub, 4).transpose(1, 0, 2, 3).reshape(groups * half_tok, 4)

        d_x_norm = _d_norm(logits, meta_own, w_head)
        d_x_norm = lax.psum(d_x_norm, 'tp')
        cols = vocab_local // 2 // N_COL
        part_a = _d_head_first(x_a, meta_a, w_head, cols)
        d_head = _d_head_last(x_b, meta_b, w_head, part_a, cols)
        d_hidden, d_gain = _finish(hidden_rows, d_x_norm, gain)
        d_gain = lax.psum(d_gain.reshape(width), ('cp', 'dp'))
        return tok_loss, loss_mean, d_hidden.reshape(hidden.shape), d_gain, d_head

    return jax.shard_map(part_fn, mesh=mesh, in_specs=(P('dp', 'cp', None), P('dp', 'cp'), P('dp'), P(None), P(None, 'tp')), out_specs=(P('dp', 'cp'), P(), P('dp', 'cp', None), P(None), P(None, 'tp')), check_vma=False)
```

time: 1710 us -> 1110 us (0.65)
  waiting for transfers between devices: 1320 us -> 310 us
  Pallas kernels: 0 us -> 631 us
  matrix products: 196 us -> 0 us
  other arithmetic: 42.4 us -> 2.87 us
    psum x2 -> x1, waiting for transfers between devices: 1320 us -> 310 us  [part_fn(): d_x_norm = lax.psum(d_x_norm, 'tp')]
    pallas_call x0 -> x6, Pallas kernels: none -> 631 us  [the longest x1 244 us: _d_head_last(): pl.pallas_call(kernel, grid=(n_col, n_tok), out_shape=jax.ShapeDtypeStruc...]
    dot_general x3 -> x0, matrix products: 196 us -> none  [the longest x1 70.3 us: local_fn(): jnp.einsum('bsd,bsv->dv', x_norm, d_logits, preferred_element_type=jnp.fl...]
    all_gather x0 -> x1, blocking collectives: none -> 44.5 us  [part_fn(): lax.all_gather(mine, ('tp', 'cp', 'dp'), axis=0, tiled=False)]
    reduce_sum x5 -> x2, other arithmetic: 34.6 us -> 0.65 us  [the longest x1 0.62 us: part_fn(): loss_mean = jnp.sum(all_loss) / valid_count]
    psum x3 -> x1, blocking collectives: 33.9 us -> 13.7 us  [part_fn(): d_gain = lax.psum(d_gain.reshape(width), ('cp', 'dp'))]
    unnamed x9 -> x1, local copies, waits for them, and re-layouts: 65.7 us -> 65.4 us
  transfers between devices with their start and end apart: 4 -> 4, of which waited for: 2 -> 1; matrix products, arithmetic and copies ran while one was open for 9% -> 1% of each run, Pallas kernels for 0% -> 23%
where the time goes in v1:
time: 1110 us
  Pallas kernels  631 us (57%)
  waiting for transfers between devices  310 us (28%)
  local copies, waits for them, and re-layouts  84.1 us (8%)
  blocking collectives  58.2 us (5%)
  between operations  18.1 us (2%)
    psum x1, waiting for transfers between devices, part_fn(): d_x_norm = lax.psum(d_x_norm, 'tp')  310 us
    pallas_call x1, Pallas kernels, _d_head_last(): pl.pallas_call(kernel, grid=(n_col, n_tok), out_shape=jax.ShapeDtypeStruc...  244 us
    pallas_call x1, Pallas kernels, _d_head_first(): pl.pallas_call(kernel, grid=(half // cols, rows // TOK), out_shape=jax.Sh...  233 us
    pallas_call x1, Pallas kernels, _d_norm(): pl.pallas_call(kernel, grid=(vocab // cols,), out_shape=jax.ShapeDtypeStr...  68.8 us
    pallas_call x1, Pallas kernels, _logits(): pl.pallas_call(kernel, grid=(steps,), out_shape=[jax.ShapeDtypeStruct((ro...  68.3 us
    unnamed x1, local copies, waits for them, and re-layouts  65.4 us
    all_gather x1, blocking collectives, part_fn(): lax.all_gather(mine, ('tp', 'cp', 'dp'), axis=0, tiled=False)  44.5 us
  transfers between devices with their start and end apart: 4, of which 1 were waited for; matrix products, arithmetic and copies ran while one was open for 1% of the time, Pallas kernels for 23%

profile of v1, /device:TPU:1, one launch (start us, length us, event | category | flops | bytes accessed | tf_op | source)
XLA Modules:
  0.0 1106.1 jit_solution(4649828778166981056)
XLA Ops:
  8.0 1.0 slice_reduce_fusion.3
  9.0 2.1 collective-permute-start
  11.2 0.9 fusion.8
  12.1 0.7 compare_convert_fusion
  12.8 0.1 reshape.141
  12.9 7.9 shard_map.92
  20.9 0.1 copy.28
  21.0 0.1 copy.29
  21.0 0.1 broadcast_subtract_fusion
  21.2 1.3 sub.37.lab_ref
  22.6 68.3 %shard_map.93 = (f32[1024,12288]{1,0:T(8,128)}, f32[1024,128]{1,0:T(8,128)}) custom-call(bf16[1024,2048]{1,0:T(8,128)(2,1)} %get-tuple-element.11.x_ref, s32[1024,1]{1,0:T(8,128)} %sub.37.lab_ref, bf16[2048,12288]{1,0:T(8,128)(2,1)} %w_ref.7), custom_call_target="tpu_custom_call" | custom-call | flops 51539607552 | bytes 100663296 | tf_op jit(solution)/shard_map/pallas_call | solution.py:85
  90.9 1.1 slice_bitcast_fusion
  92.0 0.2 copy.31
  92.2 44.5 %all-gather.1 = f32[32,5,1024]{2,1,0:T(8,128)S(1)} all-gather(f32[1,5,1024]{2,1,0:T(8,128)S(1)} %maximum_bitcast_fusion), channel_id=2, replica_groups=mesh['tp'=4,'cp'=2,'dp'=4] {'tp','cp','dp'}, dimensions={0}, use_global_device_ids=true | all-gather | bytes 675840 | tf_op jit(solution)/shard_map/all_gather | solution.py:306
  136.7 0.4 copy.37
  137.1 0.6 slice_bitcast_fusion.2
  137.8 0.7 broadcast_divide_fusion
  138.4 0.6 fusion.6
  139.1 1.0 copy.33
  140.1 68.8 %shard_map.94 = f32[1024,2048]{1,0:T(8,128)} custom-call(f32[1024,12288]{1,0:T(8,128)} %get-tuple-element.13.z_ref, f32[1024,4]{1,0:T(8,128)} %bitcast.53, bf16[2048,12288]{1,0:T(8,128)(2,1)} %w_ref.7), custom_call_target="tpu_custom_call" | custom-call | flops 51539607552 | bytes 100663296 | tf_op jit(solution)/shard_map/pallas_call | solution.py:118
  208.9 0.2 all-gather.7.cloned.1.call-start
  209.2 5.5 slice.52
  214.7 2.3 constant_dynamic-slice_fusion
  217.1 0.7 reshape.135
  219.1 2.0 copy.34
  221.1 2.0 copy.35
  223.1 309.8 %all-reduce.2.cloned.1.call-done.d_ref = f32[1024,2048]{1,0:T(8,128)} async-done(((f32[1024,2048]{1,0:T(8,128)}), f32[1024,2048]{1,0:T(8,128)}) %all-reduce.2.cloned.1.call-update) | async-done | bytes 8388624 | tf_op jit(solution)/shard_map/psum | solution.py:321
  532.9 9.1 shard_map.95
  542.0 13.7 %psum.15 = f32[2048]{0:T(1024)} all-reduce(f32[2048]{0:T(1024)} %bitcast.57), channel_id=1, replica_groups=mesh['tp'=4,'cp'=2,'dp'=4] {'cp','dp'}, use_global_device_ids=true, to_apply=%region_6.7 | all-reduce | flops 2048 | bytes 16384 | tf_op jit(solution)/shard_map/psum | solution.py:326
  555.7 232.5 %shard_map.96.init_ref = f32[2048,6144]{1,0:T(8,128)} custom-call(f32[4096,2048]{1,0:T(8,128)} %all-gather.7.cloned.1.call-done.x_ref, f32[4096,4]{1,0:T(8,128)} %bitcast.52, bf16[2048,12288]{1,0:T(8,128)(2,1)} %w_ref.7), custom_call_target="tpu_custom_call" | custom-call | flops 206158430208 | bytes 268435456 | tf_op jit(solution)/shard_map/pallas_call | solution.py:145
  788.2 243.9 %shard_map.97 = f32[2048,12288]{1,0:T(8,128)} custom-call(f32[4096,2048]{1,0:T(8,128)} %all-gather.5.cloned.1.call-done.x_ref, f32[4096,4]{1,0:T(8,128)} %bitcast.51, bf16[2048,12288]{1,0:T(8,128)(2,1)} %w_ref.7, f32[2048,6144]{1,0:T(8,128)} %shard_map.96.init_ref), custom_call_target="tpu_custom_call" | custom-call | flops 206158430208 | bytes 268435456 | tf_op jit(solution)/shard_map/pallas_call | solution.py:228
  1032.2 65.4 %copy.40 = f32[2048,12288]{1,0:T(8,128)} copy(f32[2048,12288]{1,0:T(8,128)} %shard_map.97) | data formatting | bytes 201326592
  (23 shorter events, 0.5 us)
Async XLA Ops:
  8.0 524.9 %all-reduce.2.cloned.1.call-start = ((), (), s32[]{:S(2)}) async-start(), calls=%async_computation | async-start | bytes 16777216 | tf_op jit(solution)/shard_map/psum | solution.py:321
  9.0 11.8 %collective-permute-start = (s32[32]{0:T(128)S(1)}, s32[32]{0:T(128)S(1)}, u32[]{:S(2)}, u32[]{:S(2)}) collective-permute-start(s32[32]{0:T(128)S(1)} %broadcast_select_fusion.2), channel_id=1, source_target_pairs={{0,4},{4,0},{1,5},{5,1},{2,6},{6,2},{3,7},{7,3},{8,12},{12,8},{9,1... | collective-permute-start | bytes 392 | tf_op jit(solution)/shard_map/ppermute | solution.py:294
  208.9 346.8 %all-gather.7.cloned.1.call-start = ((), (), s32[]{:S(2)}) async-start(), calls=%async_computation.2 | async-start | bytes 37748736 | tf_op jit(solution)/shard_map/all_gather | solution.py:291
  214.6 573.6 %all-gather.5.cloned.1.call-start = ((), (), s32[]{:S(2)}) async-start(), calls=%async_computation.1 | async-start | bytes 34603008 | tf_op jit(solution)/shard_map/all_gather | solution.py:292
Sparse Core Ops, SparseCore 0:
  209.0 323.8 all-reduce.1
Sparse Core Ops, SparseCore 1:
  214.7 156.5 all-gather.6
  374.0 293.3 all-gather.4
